TPU v7x, 32 devices: a whole 2x2x4 slice. The times are simulated.
32 devices in a mesh: group: 2 (over core), gx: 4 (over y, x), gy: 4 (over z).
Axes of the slice: x: 2, y: 2, z: 4, core: 2. Of those that a mesh axis runs over, the one named last changes fastest.
Arguments:
- forcing: float32 [2, 80, 32, 1024], P('group', None, 'gx', 'gy'), may hold values from -24 to 24
- conduct: bfloat16 [2, 80, 32, 1024], P('group', None, 'gx', 'gy'), may hold values from 0.25 to 4
- diag_add: bfloat16 [2, 80, 32, 1024], P('group', None, 'gx', 'gy'), may hold values from 0.049804688 to 0.5
- ice_mask: int32 [32, 1024], P('gx', 'gy'), may hold values 0 or 1
- grounded: int32 [32, 1024], P('gx', 'gy'), may hold values 0 or 1
Outputs:
- solution: float32 [2, 80, 32, 1024], P('group', None, 'gx', 'gy')
- residual: float32 [2, 80, 32, 1024], P('group', None, 'gx', 'gy')
All inputs are finite; a program needn't handle non-finite values. No bound on the sum of `ice_mask` or of `grounded` on one device may be relied on, other than what follows from the above.
Results may differ from a plain program's by a relative error of at most 0.0003.
Values sent between devices are 32-bit elements; how exact they have to be, the bound alone decides.
No kernel may reach another device: no remote copies, remote signals or barrier semaphores. Data moves between devices by JAX's collectives and lax.ppermute only.
A program may use at most 64 MiB of HBM per device.

v0:
```python
import jax
import jax.numpy as jnp
from jax import lax
from jax.sharding import PartitionSpec as P

ITERS = 6
far_weight = 0.25
cross_weight = 0.5
vertical_weight = 4.0
friction_gain = 8.0
NEIGHBOURS = (
    (1, 0, 1.0),
    (-1, 0, 1.0),
    (0, 1, 1.0),
    (0, -1, 1.0),
    (2, 0, far_weight),
    (-2, 0, far_weight),
    (0, 2, far_weight),
    (0, -2, far_weight),
    (1, 1, cross_weight),
    (1, -1, cross_weight),
    (-1, 1, cross_weight),
    (-1, -1, cross_weight),
)


def with_halo(block, sides, width):
    for axis, dim in sides:
        count = lax.axis_size(axis)
        forward = [(i, i + 1) for i in range(count - 1)]
        backward = [(target, source) for source, target in forward]
        low = lax.ppermute(
            lax.slice_in_dim(block, block.shape[dim] - width, None, axis=dim), axis, forward
        )
        high = lax.ppermute(lax.slice_in_dim(block, 0, width, axis=dim), axis, backward)
        block = jnp.concatenate([low, block, high], axis=dim)
    return block


def from_partner(shard, axis, distance):
    return lax.ppermute(shard, axis, [(i, i ^ 1 << distance) for i in range(lax.axis_size(axis))])


def beside_sum(padded, extent_x, extent_y):
    summed = jnp.zeros((padded.shape[0], extent_x, extent_y), jnp.float32)
    for shift_x, shift_y, weight in NEIGHBOURS:
        summed = (
            summed
            + weight
            * padded[:, 2 + shift_x : 2 + shift_x + extent_x, 2 + shift_y : 2 + shift_y + extent_y]
        )
    return summed


def vertical_sum(values):
    zeroes = jnp.zeros_like(values[:1])
    return jnp.concatenate([values[1:], zeroes], 0) + jnp.concatenate([zeroes, values[:-1]], 0)


def spread_padded(padded, values):
    return beside_sum(padded, values.shape[1], values.shape[2]) + vertical_weight * vertical_sum(
        values
    )


def operate(vector, coupling, diagonal):
    scaled = coupling * vector
    padded = with_halo(scaled, (("gx", 1), ("gy", 2)), 2)
    return diagonal * vector - coupling * spread_padded(padded, scaled)


def paired_sums(residual, precond, applied):
    return lax.psum((jnp.sum(residual * precond), jnp.sum(applied * precond)), ("gx", "gy"))


def on_device(forcing, conduct, diag_add, ice_mask, grounded):
    own_force = forcing[0]
    layers = own_force.shape[0]
    group_id = lax.axis_index("group")
    is_ice = (group_id == 0).astype(jnp.float32)
    ice_cells = ice_mask.astype(jnp.float32)
    ground_cells = grounded.astype(jnp.float32)
    active = ice_cells * (1.0 - (1.0 - is_ice) * ground_cells)
    coupling = jnp.sqrt(conduct[0].astype(jnp.float32)) * active
    layer_index = lax.broadcasted_iota(jnp.int32, (layers, 1, 1), 0)
    edge_layer = jnp.where(group_id == 0, 0, layers - 1).astype(jnp.int32)
    edge_pick = (layer_index == edge_layer).astype(jnp.float32)
    bottom = (layer_index == 0).astype(jnp.float32)
    base_diag = diag_add[0].astype(jnp.float32) + bottom * (
        is_ice * friction_gain * ground_cells * ice_cells
    )
    padded_coupling = with_halo(coupling, (("gx", 1), ("gy", 2)), 2)
    diagonal = base_diag + coupling * spread_padded(padded_coupling, coupling)
    shared_value = active * jnp.mean(own_force, axis=0)
    shared_weight = lax.dynamic_index_in_dim(coupling, edge_layer, 0, keepdims=False)
    received = from_partner(jnp.stack([shared_value, shared_weight]), "group", 0)
    source = active * own_force + edge_pick * (active * received[1] * received[0])
    inverse = 1.0 / diagonal
    solution = jnp.zeros_like(source)
    residual = source
    precond = inverse * residual
    applied = operate(precond, coupling, diagonal)
    norm_now, curve = paired_sums(residual, precond, applied)
    step_size = norm_now / curve
    direction = precond
    along = applied
    for iteration in range(ITERS):
        solution = solution + step_size * direction
        residual = residual - step_size * along
        if iteration + 1 < ITERS:
            precond = inverse * residual
            applied = operate(precond, coupling, diagonal)
            norm_next, curve = paired_sums(residual, precond, applied)
            step_ratio = norm_next / norm_now
            step_size = norm_next / (curve - step_ratio * norm_next / step_size)
            direction = precond + step_ratio * direction
            along = applied + step_ratio * along
            norm_now = norm_next
    return (solution[None], residual[None])


def solution(mesh):
    in_specs = (
        P("group", None, "gx", "gy"),
        P("group", None, "gx", "gy"),
        P("group", None, "gx", "gy"),
        P("gx", "gy"),
        P("gx", "gy"),
    )
    out_specs = (P("group", None, "gx", "gy"), P("group", None, "gx", "gy"))
    return jax.shard_map(
        on_device, mesh=mesh, in_specs=in_specs, out_specs=out_specs, check_vma=False
    )
```

profile of v0, /device:TPU:0, one launch (start us, length us, event | category | flops | bytes accessed | tf_op | source)
XLA Modules:
  0.0 470.8 jit_solution(15038261008825120504)
XLA Ops:
  5.1 5.5 %collective-permute-start.2 = (f32[80,2,256]{2,1,0:T(2,128)S(1)}, f32[80,2,256]{2,1,0:T(2,128)S(1)}, u32[]{:S(2)}, u32[]{:S(2)}) collective-permute-start(f32[80,2,256]{2,1,0:T(2,128)S(1)} %get-tuple-element.103), channel_id=1, source_target_pairs={{0,4},{4,8},{8,12},{1,5},{5,9},{9,13},{2,6},{6,10},{10,14},{3,7},{... | collective-permute-start | bytes 491528 | tf_op jit(solution)/shard_map/ppermute | solution.py:32
  16.4 4.5 collective-permute-start.4
  28.6 5.2 %collective-permute-start.6 = (f32[80,2,256]{2,1,0:T(2,128)S(1)}, f32[80,2,256]{2,1,0:T(2,128)S(1)}, u32[]{:S(2)}, u32[]{:S(2)}) collective-permute-start(f32[80,2,256]{2,1,0:T(2,128)S(1)} %get-tuple-element.99), channel_id=1, source_target_pairs={{0,4},{4,8},{8,12},{1,5},{5,9},{9,13},{2,6},{6,10},{10,14},{3,7},{... | collective-permute-start | bytes 491528 | tf_op jit(solution)/shard_map/ppermute | solution.py:32
  40.7 4.8 %collective-permute-start.8 = (f32[80,12,2]{0,2,1:T(2,128)S(1)}, f32[80,12,2]{0,2,1:T(2,128)S(1)}, u32[]{:S(2)}, u32[]{:S(2)}) collective-permute-start(f32[80,12,2]{0,2,1:T(2,128)S(1)} %copy.20), channel_id=1, source_target_pairs={{0,1},{1,2},{2,3},{4,5},{5,6},{6,7},{8,9},{9,10},{10,11},{12,13},{... | collective-permute-start | bytes 23048 | tf_op jit(solution)/shard_map/ppermute | solution.py:32
  52.0 3.4 multiply_reduce_fusion.10
  55.4 46.6 %all-reduce.19 = (f32[]{:T(128)}, f32[]{:T(128)}) all-reduce(f32[]{:T(128)} %get-tuple-element.15, f32[]{:T(128)} %get-tuple-element.14), channel_id=1, replica_groups=mesh['group'=2,'gx'=4,'gy'=4] {'gx','gy'}, use_global_device_ids=true, to_apply=%region_2.3 | all-reduce | flops 2 | bytes 16 | tf_op jit(solution)/shard_map/psum | solution.py:73
  109.1 4.4 collective-permute-done.9
  117.7 4.7 %collective-permute-start.12 = (f32[80,12,2]{0,2,1:T(2,128)S(1)}, f32[80,12,2]{0,2,1:T(2,128)S(1)}, u32[]{:S(2)}, u32[]{:S(2)}) collective-permute-start(f32[80,12,2]{0,2,1:T(2,128)S(1)} %copy.24), channel_id=1, source_target_pairs={{0,1},{1,2},{2,3},{4,5},{5,6},{6,7},{8,9},{9,10},{10,11},{12,13},{... | collective-permute-start | bytes 23048 | tf_op jit(solution)/shard_map/ppermute | solution.py:32
  127.8 3.5 multiply_reduce_fusion.8
  131.3 39.4 %all-reduce.18 = (f32[]{:T(128)}, f32[]{:T(128)}) all-reduce(f32[]{:T(128)} %get-tuple-element.11, f32[]{:T(128)} %get-tuple-element.10), channel_id=1, replica_groups=mesh['group'=2,'gx'=4,'gy'=4] {'gx','gy'}, use_global_device_ids=true, to_apply=%region_6.7 | all-reduce | flops 2 | bytes 16 | tf_op jit(solution)/shard_map/psum | solution.py:73
  178.4 4.6 collective-permute-start.14
  191.3 4.5 collective-permute-start.16
  205.6 39.3 %all-reduce.17 = (f32[]{:T(128)}, f32[]{:T(128)}) all-reduce(f32[]{:T(128)} %get-tuple-element.9, f32[]{:T(128)} %get-tuple-element.8), channel_id=1, replica_groups=mesh['group'=2,'gx'=4,'gy'=4] {'gx','gy'}, use_global_device_ids=true, to_apply=%region_10.11 | all-reduce | flops 2 | bytes 16 | tf_op jit(solution)/shard_map/psum | solution.py:73
  252.8 4.6 collective-permute-start.18
  262.5 4.8 %collective-permute-start.20 = (f32[80,12,2]{0,2,1:T(2,128)S(1)}, f32[80,12,2]{0,2,1:T(2,128)S(1)}, u32[]{:S(2)}, u32[]{:S(2)}) collective-permute-start(f32[80,12,2]{0,2,1:T(2,128)S(1)} %copy.32), channel_id=1, source_target_pairs={{0,1},{1,2},{2,3},{4,5},{5,6},{6,7},{8,9},{9,10},{10,11},{12,13},{... | collective-permute-start | bytes 23048 | tf_op jit(solution)/shard_map/ppermute | solution.py:32
  270.7 3.5 multiply_reduce_fusion.4
  274.1 42.2 %all-reduce.16 = (f32[]{:T(128)}, f32[]{:T(128)}) all-reduce(f32[]{:T(128)} %get-tuple-element.7, f32[]{:T(128)} %get-tuple-element.6), channel_id=1, replica_groups=mesh['group'=2,'gx'=4,'gy'=4] {'gx','gy'}, use_global_device_ids=true, to_apply=%region_14.15 | all-reduce | flops 2 | bytes 16 | tf_op jit(solution)/shard_map/psum | solution.py:73
  323.3 4.6 collective-permute-start.22
  334.8 4.5 collective-permute-start.24
  344.8 3.4 multiply_reduce_fusion.2
  348.2 40.5 %all-reduce.15 = (f32[]{:T(128)}, f32[]{:T(128)}) all-reduce(f32[]{:T(128)} %get-tuple-element.5, f32[]{:T(128)} %get-tuple-element.4), channel_id=1, replica_groups=mesh['group'=2,'gx'=4,'gy'=4] {'gx','gy'}, use_global_device_ids=true, to_apply=%region_18.19 | all-reduce | flops 2 | bytes 16 | tf_op jit(solution)/shard_map/psum | solution.py:73
  396.8 4.6 collective-permute-start.26
  408.4 4.8 %collective-permute-start.28 = (f32[80,12,2]{0,2,1:T(2,128)S(1)}, f32[80,12,2]{0,2,1:T(2,128)S(1)}, u32[]{:S(2)}, u32[]{:S(2)}) collective-permute-start(f32[80,12,2]{0,2,1:T(2,128)S(1)} %copy.40), channel_id=1, source_target_pairs={{0,1},{1,2},{2,3},{4,5},{5,6},{6,7},{8,9},{9,10},{10,11},{12,13},{... | collective-permute-start | bytes 23048 | tf_op jit(solution)/shard_map/ppermute | solution.py:32
  422.0 40.5 %all-reduce.14 = (f32[]{:T(128)}, f32[]{:T(128)}) all-reduce(f32[]{:T(128)} %get-tuple-element.13, f32[]{:T(128)} %get-tuple-element.12), channel_id=1, replica_groups=mesh['group'=2,'gx'=4,'gy'=4] {'gx','gy'}, use_global_device_ids=true, to_apply=%region_22.23 | all-reduce | flops 2 | bytes 16 | tf_op jit(solution)/shard_map/psum | solution.py:73
  (180 shorter events, 119.3 us)
Async XLA Ops:
  3.8 9.1 %collective-permute-start.1 = (f32[80,2,256]{2,1,0:T(2,128)S(1)}, f32[80,2,256]{2,1,0:T(2,128)S(1)}, u32[]{:S(2)}, u32[]{:S(2)}) collective-permute-start(f32[80,2,256]{2,1,0:T(2,128)S(1)} %get-tuple-element.104), channel_id=1, source_target_pairs={{4,0},{8,4},{12,8},{5,1},{9,5},{13,9},{6,2},{10,6},{14,10},{7,3},{... | collective-permute-start | bytes 491528 | tf_op jit(solution)/shard_map/ppermute | solution.py:35
  5.1 8.9 %collective-permute-start.2 = (f32[80,2,256]{2,1,0:T(2,128)S(1)}, f32[80,2,256]{2,1,0:T(2,128)S(1)}, u32[]{:S(2)}, u32[]{:S(2)}) collective-permute-start(f32[80,2,256]{2,1,0:T(2,128)S(1)} %get-tuple-element.103), channel_id=1, source_target_pairs={{0,4},{4,8},{8,12},{1,5},{5,9},{9,13},{2,6},{6,10},{10,14},{3,7},{... | collective-permute-start | bytes 491528 | tf_op jit(solution)/shard_map/ppermute | solution.py:32
  10.7 10.3 %collective-permute-start = (f32[2,8,256]{2,1,0:T(8,128)S(1)}, f32[2,8,256]{2,1,0:T(8,128)S(1)}, u32[]{:S(2)}, u32[]{:S(2)}) collective-permute-start(f32[2,8,256]{2,1,0:T(8,128)S(1)} %pad_maximum_fusion.28), channel_id=1, source_target_pairs={{0,16},{16,0},{1,17},{17,1},{2,18},{18,2},{3,19},{19,3},{4,20},{20... | collective-permute-start | bytes 49160 | tf_op jit(solution)/shard_map/ppermute | solution.py:41
  27.3 7.8 %collective-permute-start.5 = (f32[80,2,256]{2,1,0:T(2,128)S(1)}, f32[80,2,256]{2,1,0:T(2,128)S(1)}, u32[]{:S(2)}, u32[]{:S(2)}) collective-permute-start(f32[80,2,256]{2,1,0:T(2,128)S(1)} %get-tuple-element.100), channel_id=1, source_target_pairs={{4,0},{8,4},{12,8},{5,1},{9,5},{13,9},{6,2},{10,6},{14,10},{7,3},{... | collective-permute-start | bytes 491528 | tf_op jit(solution)/shard_map/ppermute | solution.py:35
  28.6 8.0 %collective-permute-start.6 = (f32[80,2,256]{2,1,0:T(2,128)S(1)}, f32[80,2,256]{2,1,0:T(2,128)S(1)}, u32[]{:S(2)}, u32[]{:S(2)}) collective-permute-start(f32[80,2,256]{2,1,0:T(2,128)S(1)} %get-tuple-element.99), channel_id=1, source_target_pairs={{0,4},{4,8},{8,12},{1,5},{5,9},{9,13},{2,6},{6,10},{10,14},{3,7},{... | collective-permute-start | bytes 491528 | tf_op jit(solution)/shard_map/ppermute | solution.py:32
  39.2 7.5 %collective-permute-start.7 = (f32[80,12,2]{0,2,1:T(2,128)S(1)}, f32[80,12,2]{0,2,1:T(2,128)S(1)}, u32[]{:S(2)}, u32[]{:S(2)}) collective-permute-start(f32[80,12,2]{0,2,1:T(2,128)S(1)} %copy.18), channel_id=1, source_target_pairs={{1,0},{2,1},{3,2},{5,4},{6,5},{7,6},{9,8},{10,9},{11,10},{13,12},{... | collective-permute-start | bytes 23048 | tf_op jit(solution)/shard_map/ppermute | solution.py:35
  40.7 7.1 %collective-permute-start.8 = (f32[80,12,2]{0,2,1:T(2,128)S(1)}, f32[80,12,2]{0,2,1:T(2,128)S(1)}, u32[]{:S(2)}, u32[]{:S(2)}) collective-permute-start(f32[80,12,2]{0,2,1:T(2,128)S(1)} %copy.20), channel_id=1, source_target_pairs={{0,1},{1,2},{2,3},{4,5},{5,6},{6,7},{8,9},{9,10},{10,11},{12,13},{... | collective-permute-start | bytes 23048 | tf_op jit(solution)/shard_map/ppermute | solution.py:32
  106.3 7.2 %collective-permute-start.9 = (f32[80,2,256]{2,1,0:T(2,128)S(1)}, f32[80,2,256]{2,1,0:T(2,128)S(1)}, u32[]{:S(2)}, u32[]{:S(2)}) collective-permute-start(f32[80,2,256]{2,1,0:T(2,128)S(1)} %get-tuple-element.96), channel_id=1, source_target_pairs={{4,0},{8,4},{12,8},{5,1},{9,5},{13,9},{6,2},{10,6},{14,10},{7,3},{... | collective-permute-start | bytes 491528 | tf_op jit(solution)/shard_map/ppermute | solution.py:35
  116.2 7.4 %collective-permute-start.11 = (f32[80,12,2]{0,2,1:T(2,128)S(1)}, f32[80,12,2]{0,2,1:T(2,128)S(1)}, u32[]{:S(2)}, u32[]{:S(2)}) collective-permute-start(f32[80,12,2]{0,2,1:T(2,128)S(1)} %copy.22), channel_id=1, source_target_pairs={{1,0},{2,1},{3,2},{5,4},{6,5},{7,6},{9,8},{10,9},{11,10},{13,12},{... | collective-permute-start | bytes 23048 | tf_op jit(solution)/shard_map/ppermute | solution.py:35
  177.1 7.2 %collective-permute-start.13 = (f32[80,2,256]{2,1,0:T(2,128)S(1)}, f32[80,2,256]{2,1,0:T(2,128)S(1)}, u32[]{:S(2)}, u32[]{:S(2)}) collective-permute-start(f32[80,2,256]{2,1,0:T(2,128)S(1)} %get-tuple-element.92), channel_id=1, source_target_pairs={{4,0},{8,4},{12,8},{5,1},{9,5},{13,9},{6,2},{10,6},{14,10},{7,3},{... | collective-permute-start | bytes 491528 | tf_op jit(solution)/shard_map/ppermute | solution.py:35
  178.4 7.4 %collective-permute-start.14 = (f32[80,2,256]{2,1,0:T(2,128)S(1)}, f32[80,2,256]{2,1,0:T(2,128)S(1)}, u32[]{:S(2)}, u32[]{:S(2)}) collective-permute-start(f32[80,2,256]{2,1,0:T(2,128)S(1)} %get-tuple-element.91), channel_id=1, source_target_pairs={{0,4},{4,8},{8,12},{1,5},{5,9},{9,13},{2,6},{6,10},{10,14},{3,7},{... | collective-permute-start | bytes 491528 | tf_op jit(solution)/shard_map/ppermute | solution.py:32
  188.7 8.3 %collective-permute-start.15 = (f32[80,12,2]{0,2,1:T(2,128)S(1)}, f32[80,12,2]{0,2,1:T(2,128)S(1)}, u32[]{:S(2)}, u32[]{:S(2)}) collective-permute-start(f32[80,12,2]{0,2,1:T(2,128)S(1)} %copy.26), channel_id=1, source_target_pairs={{1,0},{2,1},{3,2},{5,4},{6,5},{7,6},{9,8},{10,9},{11,10},{13,12},{... | collective-permute-start | bytes 23048 | tf_op jit(solution)/shard_map/ppermute | solution.py:35
  191.3 6.8 %collective-permute-start.16 = (f32[80,12,2]{0,2,1:T(2,128)S(1)}, f32[80,12,2]{0,2,1:T(2,128)S(1)}, u32[]{:S(2)}, u32[]{:S(2)}) collective-permute-start(f32[80,12,2]{0,2,1:T(2,128)S(1)} %copy.28), channel_id=1, source_target_pairs={{0,1},{1,2},{2,3},{4,5},{5,6},{6,7},{8,9},{9,10},{10,11},{12,13},{... | collective-permute-start | bytes 23048 | tf_op jit(solution)/shard_map/ppermute | solution.py:32
  251.5 7.2 %collective-permute-start.17 = (f32[80,2,256]{2,1,0:T(2,128)S(1)}, f32[80,2,256]{2,1,0:T(2,128)S(1)}, u32[]{:S(2)}, u32[]{:S(2)}) collective-permute-start(f32[80,2,256]{2,1,0:T(2,128)S(1)} %get-tuple-element.88), channel_id=1, source_target_pairs={{4,0},{8,4},{12,8},{5,1},{9,5},{13,9},{6,2},{10,6},{14,10},{7,3},{... | collective-permute-start | bytes 491528 | tf_op jit(solution)/shard_map/ppermute | solution.py:35
  252.8 7.4 %collective-permute-start.18 = (f32[80,2,256]{2,1,0:T(2,128)S(1)}, f32[80,2,256]{2,1,0:T(2,128)S(1)}, u32[]{:S(2)}, u32[]{:S(2)}) collective-permute-start(f32[80,2,256]{2,1,0:T(2,128)S(1)} %get-tuple-element.87), channel_id=1, source_target_pairs={{0,4},{4,8},{8,12},{1,5},{5,9},{9,13},{2,6},{6,10},{10,14},{3,7},{... | collective-permute-start | bytes 491528 | tf_op jit(solution)/shard_map/ppermute | solution.py:32
  261.0 7.5 %collective-permute-start.19 = (f32[80,12,2]{0,2,1:T(2,128)S(1)}, f32[80,12,2]{0,2,1:T(2,128)S(1)}, u32[]{:S(2)}, u32[]{:S(2)}) collective-permute-start(f32[80,12,2]{0,2,1:T(2,128)S(1)} %copy.30), channel_id=1, source_target_pairs={{1,0},{2,1},{3,2},{5,4},{6,5},{7,6},{9,8},{10,9},{11,10},{13,12},{... | collective-permute-start | bytes 23048 | tf_op jit(solution)/shard_map/ppermute | solution.py:35
  262.5 6.3 %collective-permute-start.20 = (f32[80,12,2]{0,2,1:T(2,128)S(1)}, f32[80,12,2]{0,2,1:T(2,128)S(1)}, u32[]{:S(2)}, u32[]{:S(2)}) collective-permute-start(f32[80,12,2]{0,2,1:T(2,128)S(1)} %copy.32), channel_id=1, source_target_pairs={{0,1},{1,2},{2,3},{4,5},{5,6},{6,7},{8,9},{9,10},{10,11},{12,13},{... | collective-permute-start | bytes 23048 | tf_op jit(solution)/shard_map/ppermute | solution.py:32
  322.0 7.2 %collective-permute-start.21 = (f32[80,2,256]{2,1,0:T(2,128)S(1)}, f32[80,2,256]{2,1,0:T(2,128)S(1)}, u32[]{:S(2)}, u32[]{:S(2)}) collective-permute-start(f32[80,2,256]{2,1,0:T(2,128)S(1)} %get-tuple-element.84), channel_id=1, source_target_pairs={{4,0},{8,4},{12,8},{5,1},{9,5},{13,9},{6,2},{10,6},{14,10},{7,3},{... | collective-permute-start | bytes 491528 | tf_op jit(solution)/shard_map/ppermute | solution.py:35
  323.3 7.4 %collective-permute-start.22 = (f32[80,2,256]{2,1,0:T(2,128)S(1)}, f32[80,2,256]{2,1,0:T(2,128)S(1)}, u32[]{:S(2)}, u32[]{:S(2)}) collective-permute-start(f32[80,2,256]{2,1,0:T(2,128)S(1)} %get-tuple-element.83), channel_id=1, source_target_pairs={{0,4},{4,8},{8,12},{1,5},{5,9},{9,13},{2,6},{6,10},{10,14},{3,7},{... | collective-permute-start | bytes 491528 | tf_op jit(solution)/shard_map/ppermute | solution.py:32
  333.3 7.2 %collective-permute-start.23 = (f32[80,12,2]{0,2,1:T(2,128)S(1)}, f32[80,12,2]{0,2,1:T(2,128)S(1)}, u32[]{:S(2)}, u32[]{:S(2)}) collective-permute-start(f32[80,12,2]{0,2,1:T(2,128)S(1)} %copy.34), channel_id=1, source_target_pairs={{1,0},{2,1},{3,2},{5,4},{6,5},{7,6},{9,8},{10,9},{11,10},{13,12},{... | collective-permute-start | bytes 23048 | tf_op jit(solution)/shard_map/ppermute | solution.py:35
  395.5 7.3 %collective-permute-start.25 = (f32[80,2,256]{2,1,0:T(2,128)S(1)}, f32[80,2,256]{2,1,0:T(2,128)S(1)}, u32[]{:S(2)}, u32[]{:S(2)}) collective-permute-start(f32[80,2,256]{2,1,0:T(2,128)S(1)} %get-tuple-element.80), channel_id=1, source_target_pairs={{4,0},{8,4},{12,8},{5,1},{9,5},{13,9},{6,2},{10,6},{14,10},{7,3},{... | collective-permute-start | bytes 491528 | tf_op jit(solution)/shard_map/ppermute | solution.py:35
  396.8 7.4 %collective-permute-start.26 = (f32[80,2,256]{2,1,0:T(2,128)S(1)}, f32[80,2,256]{2,1,0:T(2,128)S(1)}, u32[]{:S(2)}, u32[]{:S(2)}) collective-permute-start(f32[80,2,256]{2,1,0:T(2,128)S(1)} %get-tuple-element.79), channel_id=1, source_target_pairs={{0,4},{4,8},{8,12},{1,5},{5,9},{9,13},{2,6},{6,10},{10,14},{3,7},{... | collective-permute-start | bytes 491528 | tf_op jit(solution)/shard_map/ppermute | solution.py:32
  406.8 7.5 %collective-permute-start.27 = (f32[80,12,2]{0,2,1:T(2,128)S(1)}, f32[80,12,2]{0,2,1:T(2,128)S(1)}, u32[]{:S(2)}, u32[]{:S(2)}) collective-permute-start(f32[80,12,2]{0,2,1:T(2,128)S(1)} %copy.38), channel_id=1, source_target_pairs={{1,0},{2,1},{3,2},{5,4},{6,5},{7,6},{9,8},{10,9},{11,10},{13,12},{... | collective-permute-start | bytes 23048 | tf_op jit(solution)/shard_map/ppermute | solution.py:35
  408.4 6.3 %collective-permute-start.28 = (f32[80,12,2]{0,2,1:T(2,128)S(1)}, f32[80,12,2]{0,2,1:T(2,128)S(1)}, u32[]{:S(2)}, u32[]{:S(2)}) collective-permute-start(f32[80,12,2]{0,2,1:T(2,128)S(1)} %copy.40), channel_id=1, source_target_pairs={{0,1},{1,2},{2,3},{4,5},{5,6},{6,7},{8,9},{9,10},{10,11},{12,13},{... | collective-permute-start | bytes 23048 | tf_op jit(solution)/shard_map/ppermute | solution.py:32
  (33 other events, 321.4 us)
where the time goes:
time: 473 us; the launch traced here: 471 us
  blocking collectives  249 us (53%)
  starting transfers between devices  81 us (17%)
  other arithmetic  59.5 us (13%)
  local copies, waits for them, and re-layouts  35.4 us (7%)
  waiting for transfers between devices  23.2 us (5%)
  between operations  23.2 us (5%)
    psum x6, blocking collectives, paired_sums(): lax.psum((jnp.sum(residual * precond), jnp.sum(applied * precond)), ('gx'...  249 us
    ppermute x14, starting transfers between devices, with_halo(): lax.ppermute(lax.slice_in_dim(block, block.shape[dim] - width, None, axis...  62.9 us
    reduce_sum x6, other arithmetic, paired_sums(): jnp.sum(applied * precond)  20.6 us
    concatenate x14, other arithmetic, with_halo(): block = jnp.concatenate([low, block, high], axis=dim)  18.5 us
    ppermute x14, starting transfers between devices, with_halo(): lax.ppermute(lax.slice_in_dim(block, 0, width, axis=dim), axis, backward)  18 us
    mul x6, other arithmetic, operate(): scaled = coupling * vector  13.2 us
    slice x14, local copies, waits for them, and re-layouts, with_halo(): lax.slice_in_dim(block, 0, width, axis=dim)  13.1 us
    ppermute x14, waiting for transfers between devices, with_halo(): lax.ppermute(lax.slice_in_dim(block, 0, width, axis=dim), axis, backward)  12.2 us
  transfers between devices with their start and end apart: 29, of which 15 were waited for; matrix products, arithmetic and copies ran while one was open for 3% of the time, Pallas kernels for 0%

commit v1 on v0

--- a/solution.py
+++ b/solution.py
@@ -70,7 +70,7 @@
 
 
 def paired_sums(residual, precond, applied):
-    return lax.psum((jnp.sum(residual * precond), jnp.sum(applied * precond)), ("gx", "gy"))
+    return lax.psum(lax.psum((jnp.sum(residual * precond), jnp.sum(applied * precond)), "gy"), "gx")
 
 
 def on_device(forcing, conduct, diag_add, ice_mask, grounded):

time: 473 us -> 361 us (0.76)
  blocking collectives: 249 us -> 137 us
    psum x6 -> x12, blocking collectives: 249 us -> 137 us  [the longest x6 69.4 us: paired_sums(): lax.psum(lax.psum((jnp.sum(residual * precond), jnp.sum(applied * precond...]
  transfers between devices with their start and end apart: 29 -> 29, of which waited for: 15 -> 15; matrix products, arithmetic and copies ran while one was open for 3% -> 4% of each run, Pallas kernels for 0% -> 0%
where the time goes in v1:
time: 361 us; the launch traced here: 359 us
  blocking collectives  137 us (38%)
  starting transfers between devices  81.6 us (23%)
  other arithmetic  59.4 us (16%)
  local copies, waits for them, and re-layouts  35.4 us (10%)
  waiting for transfers between devices  23.2 us (6%)
  between operations  22.6 us (6%)
    psum x6, blocking collectives, paired_sums(): lax.psum(lax.psum((jnp.sum(residual * precond), jnp.sum(applied * precond...  69.4 us
    psum x6, blocking collectives, paired_sums(): lax.psum((jnp.sum(residual * precond), jnp.sum(applied * precond)), 'gy')  67.4 us
    ppermute x14, starting transfers between devices, with_halo(): lax.ppermute(lax.slice_in_dim(block, block.shape[dim] - width, None, axis...  63.5 us
    reduce_sum x6, other arithmetic, paired_sums(): jnp.sum(applied * precond)  20.4 us
    concatenate x14, other arithmetic, with_halo(): block = jnp.concatenate([low, block, high], axis=dim)  18.5 us
    ppermute x14, starting transfers between devices, with_halo(): lax.ppermute(lax.slice_in_dim(block, 0, width, axis=dim), axis, backward)  18 us
    mul x6, other arithmetic, operate(): scaled = coupling * vector  13.2 us
    slice x14, local copies, waits for them, and re-layouts, with_halo(): lax.slice_in_dim(block, 0, width, axis=dim)  13 us
  transfers between devices with their start and end apart: 29, of which 15 were waited for; matrix products, arithmetic and copies ran while one was open for 4% of the time, Pallas kernels for 0%

profile of v1, /device:TPU:0, one launch (start us, length us, event | category | flops | bytes accessed | tf_op | source)
XLA Modules:
  0.0 358.9 jit_solution(3629934443591543465)
XLA Ops:
  5.1 5.5 %collective-permute-start.2 = (f32[80,2,256]{2,1,0:T(2,128)S(1)}, f32[80,2,256]{2,1,0:T(2,128)S(1)}, u32[]{:S(2)}, u32[]{:S(2)}) collective-permute-start(f32[80,2,256]{2,1,0:T(2,128)S(1)} %get-tuple-element.115), channel_id=1, source_target_pairs={{0,4},{4,8},{8,12},{1,5},{5,9},{9,13},{2,6},{6,10},{10,14},{3,7},{... | collective-permute-start | bytes 491528 | tf_op jit(solution)/shard_map/ppermute | solution.py:32
  16.4 4.5 %collective-permute-start.4 = (f32[80,12,2]{0,2,1:T(2,128)S(1)}, f32[80,12,2]{0,2,1:T(2,128)S(1)}, u32[]{:S(2)}, u32[]{:S(2)}) collective-permute-start(f32[80,12,2]{0,2,1:T(2,128)S(1)} %copy.16), channel_id=1, source_target_pairs={{0,1},{1,2},{2,3},{4,5},{5,6},{6,7},{8,9},{9,10},{10,11},{12,13},{... | collective-permute-start | bytes 23048 | tf_op jit(solution)/shard_map/ppermute | solution.py:32
  28.6 5.2 %collective-permute-start.6 = (f32[80,2,256]{2,1,0:T(2,128)S(1)}, f32[80,2,256]{2,1,0:T(2,128)S(1)}, u32[]{:S(2)}, u32[]{:S(2)}) collective-permute-start(f32[80,2,256]{2,1,0:T(2,128)S(1)} %get-tuple-element.111), channel_id=1, source_target_pairs={{0,4},{4,8},{8,12},{1,5},{5,9},{9,13},{2,6},{6,10},{10,14},{3,7},{... | collective-permute-start | bytes 491528 | tf_op jit(solution)/shard_map/ppermute | solution.py:32
  40.7 4.8 %collective-permute-start.8 = (f32[80,12,2]{0,2,1:T(2,128)S(1)}, f32[80,12,2]{0,2,1:T(2,128)S(1)}, u32[]{:S(2)}, u32[]{:S(2)}) collective-permute-start(f32[80,12,2]{0,2,1:T(2,128)S(1)} %copy.20), channel_id=1, source_target_pairs={{0,1},{1,2},{2,3},{4,5},{5,6},{6,7},{8,9},{9,10},{10,11},{12,13},{... | collective-permute-start | bytes 23048 | tf_op jit(solution)/shard_map/ppermute | solution.py:32
  55.4 13.0 %all-reduce.19 = (f32[]{:T(128)}, f32[]{:T(128)}) all-reduce(f32[]{:T(128)} %get-tuple-element.15, f32[]{:T(128)} %get-tuple-element.14), channel_id=1, replica_groups=mesh['group'=2,'gx'=4,'gy'=4] {'gy'}, use_global_device_ids=true, to_apply=%region_2.3 | all-reduce | flops 2 | bytes 16 | tf_op jit(solution)/shard_map/psum | solution.py:73
  68.3 13.9 %all-reduce.25 = (f32[]{:T(128)}, f32[]{:T(128)}) all-reduce(f32[]{:T(128)} %get-tuple-element.26, f32[]{:T(128)} %get-tuple-element.27), channel_id=1, replica_groups=mesh['group'=2,'gx'=4,'gy'=4] {'gx'}, use_global_device_ids=true, to_apply=%region_3.4 | all-reduce | flops 2 | bytes 16 | tf_op jit(solution)/shard_map/psum | solution.py:73
  98.6 4.7 %collective-permute-start.12 = (f32[80,12,2]{0,2,1:T(2,128)S(1)}, f32[80,12,2]{0,2,1:T(2,128)S(1)}, u32[]{:S(2)}, u32[]{:S(2)}) collective-permute-start(f32[80,12,2]{0,2,1:T(2,128)S(1)} %copy.24), channel_id=1, source_target_pairs={{0,1},{1,2},{2,3},{4,5},{5,6},{6,7},{8,9},{9,10},{10,11},{12,13},{... | collective-permute-start | bytes 23048 | tf_op jit(solution)/shard_map/ppermute | solution.py:32
  112.2 10.9 %all-reduce.18 = (f32[]{:T(128)}, f32[]{:T(128)}) all-reduce(f32[]{:T(128)} %get-tuple-element.11, f32[]{:T(128)} %get-tuple-element.10), channel_id=1, replica_groups=mesh['group'=2,'gx'=4,'gy'=4] {'gy'}, use_global_device_ids=true, to_apply=%region_8.9 | all-reduce | flops 2 | bytes 16 | tf_op jit(solution)/shard_map/psum | solution.py:73
  123.1 11.0 %all-reduce.24 = (f32[]{:T(128)}, f32[]{:T(128)}) all-reduce(f32[]{:T(128)} %get-tuple-element.24, f32[]{:T(128)} %get-tuple-element.25), channel_id=1, replica_groups=mesh['group'=2,'gx'=4,'gy'=4] {'gx'}, use_global_device_ids=true, to_apply=%region_9.10 | all-reduce | flops 2 | bytes 16 | tf_op jit(solution)/shard_map/psum | solution.py:73
  141.9 4.6 %collective-permute-start.14 = (f32[80,2,256]{2,1,0:T(2,128)S(1)}, f32[80,2,256]{2,1,0:T(2,128)S(1)}, u32[]{:S(2)}, u32[]{:S(2)}) collective-permute-start(f32[80,2,256]{2,1,0:T(2,128)S(1)} %get-tuple-element.103), channel_id=1, source_target_pairs={{0,4},{4,8},{8,12},{1,5},{5,9},{9,13},{2,6},{6,10},{10,14},{3,7},{... | collective-permute-start | bytes 491528 | tf_op jit(solution)/shard_map/ppermute | solution.py:32
  168.9 10.4 %all-reduce.17 = (f32[]{:T(128)}, f32[]{:T(128)}) all-reduce(f32[]{:T(128)} %get-tuple-element.9, f32[]{:T(128)} %get-tuple-element.8), channel_id=1, replica_groups=mesh['group'=2,'gx'=4,'gy'=4] {'gy'}, use_global_device_ids=true, to_apply=%region_14.15 | all-reduce | flops 2 | bytes 16 | tf_op jit(solution)/shard_map/psum | solution.py:73
  179.3 11.6 %all-reduce.23 = (f32[]{:T(128)}, f32[]{:T(128)}) all-reduce(f32[]{:T(128)} %get-tuple-element.22, f32[]{:T(128)} %get-tuple-element.23), channel_id=1, replica_groups=mesh['group'=2,'gx'=4,'gy'=4] {'gx'}, use_global_device_ids=true, to_apply=%region_15.16 | all-reduce | flops 2 | bytes 16 | tf_op jit(solution)/shard_map/psum | solution.py:73
  198.7 4.6 %collective-permute-start.18 = (f32[80,2,256]{2,1,0:T(2,128)S(1)}, f32[80,2,256]{2,1,0:T(2,128)S(1)}, u32[]{:S(2)}, u32[]{:S(2)}) collective-permute-start(f32[80,2,256]{2,1,0:T(2,128)S(1)} %get-tuple-element.99), channel_id=1, source_target_pairs={{0,4},{4,8},{8,12},{1,5},{5,9},{9,13},{2,6},{6,10},{10,14},{3,7},{... | collective-permute-start | bytes 491528 | tf_op jit(solution)/shard_map/ppermute | solution.py:32
  208.4 4.8 %collective-permute-start.20 = (f32[80,12,2]{0,2,1:T(2,128)S(1)}, f32[80,12,2]{0,2,1:T(2,128)S(1)}, u32[]{:S(2)}, u32[]{:S(2)}) collective-permute-start(f32[80,12,2]{0,2,1:T(2,128)S(1)} %copy.32), channel_id=1, source_target_pairs={{0,1},{1,2},{2,3},{4,5},{5,6},{6,7},{8,9},{9,10},{10,11},{12,13},{... | collective-permute-start | bytes 23048 | tf_op jit(solution)/shard_map/ppermute | solution.py:32
  220.0 11.0 %all-reduce.16 = (f32[]{:T(128)}, f32[]{:T(128)}) all-reduce(f32[]{:T(128)} %get-tuple-element.7, f32[]{:T(128)} %get-tuple-element.6), channel_id=1, replica_groups=mesh['group'=2,'gx'=4,'gy'=4] {'gy'}, use_global_device_ids=true, to_apply=%region_20.21 | all-reduce | flops 2 | bytes 16 | tf_op jit(solution)/shard_map/psum | solution.py:73
  230.9 10.6 %all-reduce.22 = (f32[]{:T(128)}, f32[]{:T(128)}) all-reduce(f32[]{:T(128)} %get-tuple-element.20, f32[]{:T(128)} %get-tuple-element.21), channel_id=1, replica_groups=mesh['group'=2,'gx'=4,'gy'=4] {'gx'}, use_global_device_ids=true, to_apply=%region_21.22 | all-reduce | flops 2 | bytes 16 | tf_op jit(solution)/shard_map/psum | solution.py:73
  248.4 4.6 %collective-permute-start.22 = (f32[80,2,256]{2,1,0:T(2,128)S(1)}, f32[80,2,256]{2,1,0:T(2,128)S(1)}, u32[]{:S(2)}, u32[]{:S(2)}) collective-permute-start(f32[80,2,256]{2,1,0:T(2,128)S(1)} %get-tuple-element.95), channel_id=1, source_target_pairs={{0,4},{4,8},{8,12},{1,5},{5,9},{9,13},{2,6},{6,10},{10,14},{3,7},{... | collective-permute-start | bytes 491528 | tf_op jit(solution)/shard_map/ppermute | solution.py:32
  260.0 4.5 %collective-permute-start.24 = (f32[80,12,2]{0,2,1:T(2,128)S(1)}, f32[80,12,2]{0,2,1:T(2,128)S(1)}, u32[]{:S(2)}, u32[]{:S(2)}) collective-permute-start(f32[80,12,2]{0,2,1:T(2,128)S(1)} %copy.36), channel_id=1, source_target_pairs={{0,1},{1,2},{2,3},{4,5},{5,6},{6,7},{8,9},{9,10},{10,11},{12,13},{... | collective-permute-start | bytes 23048 | tf_op jit(solution)/shard_map/ppermute | solution.py:32
  273.3 11.2 %all-reduce.15 = (f32[]{:T(128)}, f32[]{:T(128)}) all-reduce(f32[]{:T(128)} %get-tuple-element.5, f32[]{:T(128)} %get-tuple-element.4), channel_id=1, replica_groups=mesh['group'=2,'gx'=4,'gy'=4] {'gy'}, use_global_device_ids=true, to_apply=%region_26.27 | all-reduce | flops 2 | bytes 16 | tf_op jit(solution)/shard_map/psum | solution.py:73
  284.4 11.5 %all-reduce.21 = (f32[]{:T(128)}, f32[]{:T(128)}) all-reduce(f32[]{:T(128)} %get-tuple-element.18, f32[]{:T(128)} %get-tuple-element.19), channel_id=1, replica_groups=mesh['group'=2,'gx'=4,'gy'=4] {'gx'}, use_global_device_ids=true, to_apply=%region_27.28 | all-reduce | flops 2 | bytes 16 | tf_op jit(solution)/shard_map/psum | solution.py:73
  303.9 4.6 %collective-permute-start.26 = (f32[80,2,256]{2,1,0:T(2,128)S(1)}, f32[80,2,256]{2,1,0:T(2,128)S(1)}, u32[]{:S(2)}, u32[]{:S(2)}) collective-permute-start(f32[80,2,256]{2,1,0:T(2,128)S(1)} %get-tuple-element.91), channel_id=1, source_target_pairs={{0,4},{4,8},{8,12},{1,5},{5,9},{9,13},{2,6},{6,10},{10,14},{3,7},{... | collective-permute-start | bytes 491528 | tf_op jit(solution)/shard_map/ppermute | solution.py:32
  315.5 4.8 %collective-permute-start.28 = (f32[80,12,2]{0,2,1:T(2,128)S(1)}, f32[80,12,2]{0,2,1:T(2,128)S(1)}, u32[]{:S(2)}, u32[]{:S(2)}) collective-permute-start(f32[80,12,2]{0,2,1:T(2,128)S(1)} %copy.40), channel_id=1, source_target_pairs={{0,1},{1,2},{2,3},{4,5},{5,6},{6,7},{8,9},{9,10},{10,11},{12,13},{... | collective-permute-start | bytes 23048 | tf_op jit(solution)/shard_map/ppermute | solution.py:32
  329.1 10.9 %all-reduce.14 = (f32[]{:T(128)}, f32[]{:T(128)}) all-reduce(f32[]{:T(128)} %get-tuple-element.13, f32[]{:T(128)} %get-tuple-element.12), channel_id=1, replica_groups=mesh['group'=2,'gx'=4,'gy'=4] {'gy'}, use_global_device_ids=true, to_apply=%region_32.33 | all-reduce | flops 2 | bytes 16 | tf_op jit(solution)/shard_map/psum | solution.py:73
  340.1 10.7 %all-reduce.20 = (f32[]{:T(128)}, f32[]{:T(128)}) all-reduce(f32[]{:T(128)} %get-tuple-element.16, f32[]{:T(128)} %get-tuple-element.17), channel_id=1, replica_groups=mesh['group'=2,'gx'=4,'gy'=4] {'gx'}, use_global_device_ids=true, to_apply=%region_33.34 | all-reduce | flops 2 | bytes 16 | tf_op jit(solution)/shard_map/psum | solution.py:73
  (186 shorter events, 142.5 us)
Async XLA Ops:
  3.8 9.1 %collective-permute-start.1 = (f32[80,2,256]{2,1,0:T(2,128)S(1)}, f32[80,2,256]{2,1,0:T(2,128)S(1)}, u32[]{:S(2)}, u32[]{:S(2)}) collective-permute-start(f32[80,2,256]{2,1,0:T(2,128)S(1)} %get-tuple-element.116), channel_id=1, source_target_pairs={{4,0},{8,4},{12,8},{5,1},{9,5},{13,9},{6,2},{10,6},{14,10},{7,3},{... | collective-permute-start | bytes 491528 | tf_op jit(solution)/shard_map/ppermute | solution.py:35
  5.1 8.9 %collective-permute-start.2 = (f32[80,2,256]{2,1,0:T(2,128)S(1)}, f32[80,2,256]{2,1,0:T(2,128)S(1)}, u32[]{:S(2)}, u32[]{:S(2)}) collective-permute-start(f32[80,2,256]{2,1,0:T(2,128)S(1)} %get-tuple-element.115), channel_id=1, source_target_pairs={{0,4},{4,8},{8,12},{1,5},{5,9},{9,13},{2,6},{6,10},{10,14},{3,7},{... | collective-permute-start | bytes 491528 | tf_op jit(solution)/shard_map/ppermute | solution.py:32
  10.7 10.3 %collective-permute-start = (f32[2,8,256]{2,1,0:T(8,128)S(1)}, f32[2,8,256]{2,1,0:T(8,128)S(1)}, u32[]{:S(2)}, u32[]{:S(2)}) collective-permute-start(f32[2,8,256]{2,1,0:T(8,128)S(1)} %pad_maximum_fusion.28), channel_id=1, source_target_pairs={{0,16},{16,0},{1,17},{17,1},{2,18},{18,2},{3,19},{19,3},{4,20},{20... | collective-permute-start | bytes 49160 | tf_op jit(solution)/shard_map/ppermute | solution.py:41
  27.3 7.8 %collective-permute-start.5 = (f32[80,2,256]{2,1,0:T(2,128)S(1)}, f32[80,2,256]{2,1,0:T(2,128)S(1)}, u32[]{:S(2)}, u32[]{:S(2)}) collective-permute-start(f32[80,2,256]{2,1,0:T(2,128)S(1)} %get-tuple-element.112), channel_id=1, source_target_pairs={{4,0},{8,4},{12,8},{5,1},{9,5},{13,9},{6,2},{10,6},{14,10},{7,3},{... | collective-permute-start | bytes 491528 | tf_op jit(solution)/shard_map/ppermute | solution.py:35
  28.6 8.0 %collective-permute-start.6 = (f32[80,2,256]{2,1,0:T(2,128)S(1)}, f32[80,2,256]{2,1,0:T(2,128)S(1)}, u32[]{:S(2)}, u32[]{:S(2)}) collective-permute-start(f32[80,2,256]{2,1,0:T(2,128)S(1)} %get-tuple-element.111), channel_id=1, source_target_pairs={{0,4},{4,8},{8,12},{1,5},{5,9},{9,13},{2,6},{6,10},{10,14},{3,7},{... | collective-permute-start | bytes 491528 | tf_op jit(solution)/shard_map/ppermute | solution.py:32
  39.2 7.5 %collective-permute-start.7 = (f32[80,12,2]{0,2,1:T(2,128)S(1)}, f32[80,12,2]{0,2,1:T(2,128)S(1)}, u32[]{:S(2)}, u32[]{:S(2)}) collective-permute-start(f32[80,12,2]{0,2,1:T(2,128)S(1)} %copy.18), channel_id=1, source_target_pairs={{1,0},{2,1},{3,2},{5,4},{6,5},{7,6},{9,8},{10,9},{11,10},{13,12},{... | collective-permute-start | bytes 23048 | tf_op jit(solution)/shard_map/ppermute | solution.py:35
  40.7 7.1 %collective-permute-start.8 = (f32[80,12,2]{0,2,1:T(2,128)S(1)}, f32[80,12,2]{0,2,1:T(2,128)S(1)}, u32[]{:S(2)}, u32[]{:S(2)}) collective-permute-start(f32[80,12,2]{0,2,1:T(2,128)S(1)} %copy.20), channel_id=1, source_target_pairs={{0,1},{1,2},{2,3},{4,5},{5,6},{6,7},{8,9},{9,10},{10,11},{12,13},{... | collective-permute-start | bytes 23048 | tf_op jit(solution)/shard_map/ppermute | solution.py:32
  87.2 7.2 %collective-permute-start.9 = (f32[80,2,256]{2,1,0:T(2,128)S(1)}, f32[80,2,256]{2,1,0:T(2,128)S(1)}, u32[]{:S(2)}, u32[]{:S(2)}) collective-permute-start(f32[80,2,256]{2,1,0:T(2,128)S(1)} %get-tuple-element.108), channel_id=1, source_target_pairs={{4,0},{8,4},{12,8},{5,1},{9,5},{13,9},{6,2},{10,6},{14,10},{7,3},{... | collective-permute-start | bytes 491528 | tf_op jit(solution)/shard_map/ppermute | solution.py:35
  97.0 7.4 %collective-permute-start.11 = (f32[80,12,2]{0,2,1:T(2,128)S(1)}, f32[80,12,2]{0,2,1:T(2,128)S(1)}, u32[]{:S(2)}, u32[]{:S(2)}) collective-permute-start(f32[80,12,2]{0,2,1:T(2,128)S(1)} %copy.22), channel_id=1, source_target_pairs={{1,0},{2,1},{3,2},{5,4},{6,5},{7,6},{9,8},{10,9},{11,10},{13,12},{... | collective-permute-start | bytes 23048 | tf_op jit(solution)/shard_map/ppermute | solution.py:35
  140.6 7.2 %collective-permute-start.13 = (f32[80,2,256]{2,1,0:T(2,128)S(1)}, f32[80,2,256]{2,1,0:T(2,128)S(1)}, u32[]{:S(2)}, u32[]{:S(2)}) collective-permute-start(f32[80,2,256]{2,1,0:T(2,128)S(1)} %get-tuple-element.104), channel_id=1, source_target_pairs={{4,0},{8,4},{12,8},{5,1},{9,5},{13,9},{6,2},{10,6},{14,10},{7,3},{... | collective-permute-start | bytes 491528 | tf_op jit(solution)/shard_map/ppermute | solution.py:35
  141.9 7.4 %collective-permute-start.14 = (f32[80,2,256]{2,1,0:T(2,128)S(1)}, f32[80,2,256]{2,1,0:T(2,128)S(1)}, u32[]{:S(2)}, u32[]{:S(2)}) collective-permute-start(f32[80,2,256]{2,1,0:T(2,128)S(1)} %get-tuple-element.103), channel_id=1, source_target_pairs={{0,4},{4,8},{8,12},{1,5},{5,9},{9,13},{2,6},{6,10},{10,14},{3,7},{... | collective-permute-start | bytes 491528 | tf_op jit(solution)/shard_map/ppermute | solution.py:32
  152.1 8.3 %collective-permute-start.15 = (f32[80,12,2]{0,2,1:T(2,128)S(1)}, f32[80,12,2]{0,2,1:T(2,128)S(1)}, u32[]{:S(2)}, u32[]{:S(2)}) collective-permute-start(f32[80,12,2]{0,2,1:T(2,128)S(1)} %copy.26), channel_id=1, source_target_pairs={{1,0},{2,1},{3,2},{5,4},{6,5},{7,6},{9,8},{10,9},{11,10},{13,12},{... | collective-permute-start | bytes 23048 | tf_op jit(solution)/shard_map/ppermute | solution.py:35
  154.7 6.9 %collective-permute-start.16 = (f32[80,12,2]{0,2,1:T(2,128)S(1)}, f32[80,12,2]{0,2,1:T(2,128)S(1)}, u32[]{:S(2)}, u32[]{:S(2)}) collective-permute-start(f32[80,12,2]{0,2,1:T(2,128)S(1)} %copy.28), channel_id=1, source_target_pairs={{0,1},{1,2},{2,3},{4,5},{5,6},{6,7},{8,9},{9,10},{10,11},{12,13},{... | collective-permute-start | bytes 23048 | tf_op jit(solution)/shard_map/ppermute | solution.py:32
  197.4 7.2 %collective-permute-start.17 = (f32[80,2,256]{2,1,0:T(2,128)S(1)}, f32[80,2,256]{2,1,0:T(2,128)S(1)}, u32[]{:S(2)}, u32[]{:S(2)}) collective-permute-start(f32[80,2,256]{2,1,0:T(2,128)S(1)} %get-tuple-element.100), channel_id=1, source_target_pairs={{4,0},{8,4},{12,8},{5,1},{9,5},{13,9},{6,2},{10,6},{14,10},{7,3},{... | collective-permute-start | bytes 491528 | tf_op jit(solution)/shard_map/ppermute | solution.py:35
  198.7 7.4 %collective-permute-start.18 = (f32[80,2,256]{2,1,0:T(2,128)S(1)}, f32[80,2,256]{2,1,0:T(2,128)S(1)}, u32[]{:S(2)}, u32[]{:S(2)}) collective-permute-start(f32[80,2,256]{2,1,0:T(2,128)S(1)} %get-tuple-element.99), channel_id=1, source_target_pairs={{0,4},{4,8},{8,12},{1,5},{5,9},{9,13},{2,6},{6,10},{10,14},{3,7},{... | collective-permute-start | bytes 491528 | tf_op jit(solution)/shard_map/ppermute | solution.py:32
  206.8 7.5 %collective-permute-start.19 = (f32[80,12,2]{0,2,1:T(2,128)S(1)}, f32[80,12,2]{0,2,1:T(2,128)S(1)}, u32[]{:S(2)}, u32[]{:S(2)}) collective-permute-start(f32[80,12,2]{0,2,1:T(2,128)S(1)} %copy.30), channel_id=1, source_target_pairs={{1,0},{2,1},{3,2},{5,4},{6,5},{7,6},{9,8},{10,9},{11,10},{13,12},{... | collective-permute-start | bytes 23048 | tf_op jit(solution)/shard_map/ppermute | solution.py:35
  208.4 6.3 %collective-permute-start.20 = (f32[80,12,2]{0,2,1:T(2,128)S(1)}, f32[80,12,2]{0,2,1:T(2,128)S(1)}, u32[]{:S(2)}, u32[]{:S(2)}) collective-permute-start(f32[80,12,2]{0,2,1:T(2,128)S(1)} %copy.32), channel_id=1, source_target_pairs={{0,1},{1,2},{2,3},{4,5},{5,6},{6,7},{8,9},{9,10},{10,11},{12,13},{... | collective-permute-start | bytes 23048 | tf_op jit(solution)/shard_map/ppermute | solution.py:32
  247.1 7.2 %collective-permute-start.21 = (f32[80,2,256]{2,1,0:T(2,128)S(1)}, f32[80,2,256]{2,1,0:T(2,128)S(1)}, u32[]{:S(2)}, u32[]{:S(2)}) collective-permute-start(f32[80,2,256]{2,1,0:T(2,128)S(1)} %get-tuple-element.96), channel_id=1, source_target_pairs={{4,0},{8,4},{12,8},{5,1},{9,5},{13,9},{6,2},{10,6},{14,10},{7,3},{... | collective-permute-start | bytes 491528 | tf_op jit(solution)/shard_map/ppermute | solution.py:35
  248.4 7.4 %collective-permute-start.22 = (f32[80,2,256]{2,1,0:T(2,128)S(1)}, f32[80,2,256]{2,1,0:T(2,128)S(1)}, u32[]{:S(2)}, u32[]{:S(2)}) collective-permute-start(f32[80,2,256]{2,1,0:T(2,128)S(1)} %get-tuple-element.95), channel_id=1, source_target_pairs={{0,4},{4,8},{8,12},{1,5},{5,9},{9,13},{2,6},{6,10},{10,14},{3,7},{... | collective-permute-start | bytes 491528 | tf_op jit(solution)/shard_map/ppermute | solution.py:32
  258.4 7.2 %collective-permute-start.23 = (f32[80,12,2]{0,2,1:T(2,128)S(1)}, f32[80,12,2]{0,2,1:T(2,128)S(1)}, u32[]{:S(2)}, u32[]{:S(2)}) collective-permute-start(f32[80,12,2]{0,2,1:T(2,128)S(1)} %copy.34), channel_id=1, source_target_pairs={{1,0},{2,1},{3,2},{5,4},{6,5},{7,6},{9,8},{10,9},{11,10},{13,12},{... | collective-permute-start | bytes 23048 | tf_op jit(solution)/shard_map/ppermute | solution.py:35
  302.6 7.3 %collective-permute-start.25 = (f32[80,2,256]{2,1,0:T(2,128)S(1)}, f32[80,2,256]{2,1,0:T(2,128)S(1)}, u32[]{:S(2)}, u32[]{:S(2)}) collective-permute-start(f32[80,2,256]{2,1,0:T(2,128)S(1)} %get-tuple-element.92), channel_id=1, source_target_pairs={{4,0},{8,4},{12,8},{5,1},{9,5},{13,9},{6,2},{10,6},{14,10},{7,3},{... | collective-permute-start | bytes 491528 | tf_op jit(solution)/shard_map/ppermute | solution.py:35
  303.9 7.4 %collective-permute-start.26 = (f32[80,2,256]{2,1,0:T(2,128)S(1)}, f32[80,2,256]{2,1,0:T(2,128)S(1)}, u32[]{:S(2)}, u32[]{:S(2)}) collective-permute-start(f32[80,2,256]{2,1,0:T(2,128)S(1)} %get-tuple-element.91), channel_id=1, source_target_pairs={{0,4},{4,8},{8,12},{1,5},{5,9},{9,13},{2,6},{6,10},{10,14},{3,7},{... | collective-permute-start | bytes 491528 | tf_op jit(solution)/shard_map/ppermute | solution.py:32
  313.9 7.5 %collective-permute-start.27 = (f32[80,12,2]{0,2,1:T(2,128)S(1)}, f32[80,12,2]{0,2,1:T(2,128)S(1)}, u32[]{:S(2)}, u32[]{:S(2)}) collective-permute-start(f32[80,12,2]{0,2,1:T(2,128)S(1)} %copy.38), channel_id=1, source_target_pairs={{1,0},{2,1},{3,2},{5,4},{6,5},{7,6},{9,8},{10,9},{11,10},{13,12},{... | collective-permute-start | bytes 23048 | tf_op jit(solution)/shard_map/ppermute | solution.py:35
  315.5 6.3 %collective-permute-start.28 = (f32[80,12,2]{0,2,1:T(2,128)S(1)}, f32[80,12,2]{0,2,1:T(2,128)S(1)}, u32[]{:S(2)}, u32[]{:S(2)}) collective-permute-start(f32[80,12,2]{0,2,1:T(2,128)S(1)} %copy.40), channel_id=1, source_target_pairs={{0,1},{1,2},{2,3},{4,5},{5,6},{6,7},{8,9},{9,10},{10,11},{12,13},{... | collective-permute-start | bytes 23048 | tf_op jit(solution)/shard_map/ppermute | solution.py:32
  (33 other events, 250.7 us)
